TPU v7x, 128 devices: a whole 4x4x4 slice. The times are simulated.
128 devices in a mesh: row: 8 (over z, core), col: 16 (over y, x).
Axes of the slice: x: 4, y: 4, z: 4, core: 2. Of those that a mesh axis runs over, the one named last changes fastest.
Arguments:
- fine_residual: bfloat16 [16, 2097152], P(None, ('row', 'col')), may hold values from -6 to 6
- tiles_one: bfloat16 [65536, 128, 128], P(('row', 'col')), may hold values from -0.125 to 0.125
- pointers_one: int32 [32896], P(('row', 'col')), may hold values from 0 to 512, as said below
- columns_one: int32 [65536], P(('row', 'col')), may hold values from 0 to 2047, as said below
- points_one: int32 [524288], P(('col', 'row')), may hold values from 0 to 16383, as said below
- tiles_two: bfloat16 [32768, 128, 128], P(('row', 'col')), may hold values from -0.09375 to 0.09375
- pointers_two: int32 [16512], P(('row', 'col')), may hold values from 0 to 256, as said below
- columns_two: int32 [32768], P(('row', 'col')), may hold values from 0 to 255
- points_two: int32 [131072], P(('row', 'col')), may hold values from 0 to 4095, as said below
- tiles_three: bfloat16 [4096, 128, 128], P(('row', 'col')), may hold values from -0.125 to 0.125
- pointers_three: int32 [2176], P(('row', 'col')), may hold values from 0 to 32, as said below
- columns_three: int32 [4096], P(('row', 'col')), may hold values from 0 to 127
- points_three: int32 [32768], P(('col', 'row')), may hold values from 0 to 1023, as said below
Outputs:
- coarse_one: bfloat16 [16, 524288], P(None, ('col', 'row'))
- coarse_two: bfloat16 [16, 131072], P(None, ('row', 'col'))
- coarse_three: bfloat16 [16, 32768], P(None, ('col', 'row'))
Inputs may be any that keep to these rules, and one draw needn't show every extreme that they name: `pointers_one`: each tile set's 256 + 1 pointers start at 0 and never fall; the last is that set's live slot count, at most 512; some set has 512 live slots. `pointers_two`: each tile set's 128 + 1 pointers start at 0 and never fall; the last is that set's live slot count, at most 256; some set has 256 live slots. `pointers_three`: each tile set's 16 + 1 pointers start at 0 and never fall; the last is that set's live slot count, at most 32; some set has 32 live slots. `columns_one`: among the live slots of one tile set, at most 32 name block columns with the same quotient by 128; some set reaches 32. `points_one`: values are distinct within each aligned run of 4096 entries. `points_two`: values are distinct within each aligned run of 1024 entries. `points_three`: values are distinct within each aligned run of 256 entries.
All inputs are finite; a program needn't handle non-finite values.
Results may differ from a plain program's by a relative error of at most 0.0057.
Values may be sent and summed in bfloat16 or wider, within the bound.
A program may use at most 128 MiB of HBM per device.

v0:
```python
import jax
import jax.numpy as jnp
from jax import lax
from jax.sharding import PartitionSpec as P


def split_up(shard, dim, size):
    before, after = (shard.shape[:dim], shard.shape[dim + 1 :])
    return jnp.moveaxis(shard.reshape(*before, size, -1, *after), dim, 0)


def summed_on_arrival(shard, axis, dim):
    parts = split_up(shard, dim, lax.axis_size(axis))
    arrived = lax.all_to_all(parts, axis, split_axis=0, concat_axis=0, tiled=True)
    return arrived.sum(axis=0)


def joined_along(parts, dim):
    parts = jnp.moveaxis(parts, 0, dim)
    shape = parts.shape
    return parts.reshape(*shape[:dim], shape[dim] * shape[dim + 1], *shape[dim + 2 :])


def from_everyone(shard, axis):
    copies = jnp.broadcast_to(shard, (lax.axis_size(axis), *shard.shape))
    return lax.all_to_all(copies, axis, split_axis=0, concat_axis=0, tiled=True)


def gathered_copies(shard, axis, dim):
    return joined_along(from_everyone(shard, axis), dim)


def slot_layout(pointers, slot_count):
    block_count = pointers.shape[0] - 1
    positions = jnp.arange(slot_count, dtype=jnp.int32)
    is_live = positions < pointers[block_count]
    finished = jnp.sum((pointers[1:][None, :] <= positions[:, None]).astype(jnp.int32), axis=1)
    segment = jnp.where(is_live, finished, block_count)
    return (is_live, segment)


def block_sums(products, segment, block_count):
    summed = jax.ops.segment_sum(
        products, segment, num_segments=block_count + 1, indices_are_sorted=True
    )
    summed = summed[:block_count]
    return jnp.transpose(summed, (1, 0, 2)).reshape(summed.shape[1], block_count * summed.shape[2])


def group_products(tiles, fine_group, columns, segment, block_count):
    vector_count = fine_group.shape[0]
    tile_edge = tiles.shape[1]
    blocks = fine_group.reshape(vector_count, fine_group.shape[1] // tile_edge, tile_edge)
    picked = jnp.take(blocks, columns, axis=1)
    products = jnp.einsum("sij,vsj->svi", tiles, picked, preferred_element_type=jnp.float32)
    return block_sums(products, segment, block_count)


def add_points(partial_value, own_piece, points, position):
    injected = jnp.take(own_piece, points, axis=1).astype(jnp.float32)
    offset = position * points.shape[0]
    current = lax.dynamic_slice_in_dim(partial_value, offset, points.shape[0], 1)
    return lax.dynamic_update_slice_in_dim(partial_value, current + injected, offset, 1)


def on_device(
    fine_residual,
    tiles_one,
    pointers_one,
    columns_one,
    points_one,
    tiles_two,
    pointers_two,
    columns_two,
    points_two,
    tiles_three,
    pointers_three,
    columns_three,
    points_three,
):
    tile_edge = tiles_one.shape[1]
    vector_count = fine_residual.shape[0]
    slots_first = tiles_one.shape[0]
    blocks_first = pointers_one.shape[0] - 1
    live_first, segment_first = slot_layout(pointers_one, slots_first)
    peer_count = lax.axis_size("col")
    per_peer = slots_first // peer_count
    blocks_peer = fine_residual.shape[1] // tile_edge
    owner_peer = columns_one // blocks_peer
    within = columns_one % blocks_peer
    peer_ids = jnp.arange(peer_count, dtype=jnp.int32)
    peer_hits = ((owner_peer[:, None] == peer_ids[None, :]) & live_first[:, None]).astype(jnp.int32)
    peer_rank = jnp.sum(jnp.cumsum(peer_hits, axis=0) * peer_hits, axis=1) - 1
    target = jnp.where(live_first, owner_peer * per_peer + peer_rank, peer_count * per_peer)
    requests = jnp.zeros((peer_count * per_peer,), jnp.int32).at[target].set(within, mode="drop")
    requests = requests.reshape(peer_count, per_peer)
    own_blocks = jnp.transpose(
        fine_residual.reshape(vector_count, blocks_peer, tile_edge), (1, 0, 2)
    )
    found_blocks = jnp.take(
        own_blocks, lax.all_to_all(requests, "col", split_axis=0, concat_axis=0, tiled=True), axis=0
    )
    replies = lax.all_to_all(found_blocks, "col", split_axis=0, concat_axis=0, tiled=True)
    flat_replies = replies.reshape(peer_count * per_peer, vector_count, tile_edge)
    picked = jnp.take(flat_replies, jnp.minimum(target, peer_count * per_peer - 1), axis=0)
    products = jnp.einsum("sij,svj->svi", tiles_one, picked, preferred_element_type=jnp.float32)
    partial_one = block_sums(products, segment_first, blocks_first)
    partial_one = add_points(partial_one, fine_residual, points_one, lax.axis_index("row"))
    coarse_one = summed_on_arrival(partial_one, "row", 1).astype(jnp.bfloat16)
    group_one = gathered_copies(coarse_one, "row", 1)
    segment_second = slot_layout(pointers_two, tiles_two.shape[0])[1]
    partial_two = group_products(
        tiles_two, group_one, columns_two, segment_second, pointers_two.shape[0] - 1
    )
    partial_two = add_points(partial_two, coarse_one, points_two, lax.axis_index("col"))
    coarse_two = summed_on_arrival(partial_two, "col", 1).astype(jnp.bfloat16)
    group_two = gathered_copies(coarse_two, "col", 1)
    segment_third = slot_layout(pointers_three, tiles_three.shape[0])[1]
    partial_three = group_products(
        tiles_three, group_two, columns_three, segment_third, pointers_three.shape[0] - 1
    )
    partial_three = add_points(partial_three, coarse_two, points_three, lax.axis_index("row"))
    coarse_three = summed_on_arrival(partial_three, "row", 1).astype(jnp.bfloat16)
    return (coarse_one, coarse_two, coarse_three)


def solution(mesh):
    placed = (
        P(None, ("row", "col")),
        P(("row", "col"), None, None),
        P(("row", "col")),
        P(("row", "col")),
        P(("col", "row")),
        P(("row", "col"), None, None),
        P(("row", "col")),
        P(("row", "col")),
        P(("row", "col")),
        P(("row", "col"), None, None),
        P(("row", "col")),
        P(("row", "col")),
        P(("col", "row")),
    )
    return jax.shard_map(
        on_device,
        mesh=mesh,
        in_specs=placed,
        out_specs=(P(None, ("col", "row")), P(None, ("row", "col")), P(None, ("col", "row"))),
        check_vma=False,
    )
```

profile of v0, /device:TPU:1, one launch (start us, length us, event | category | flops | bytes accessed | tf_op | source)
XLA Modules:
  0.0 274.6 jit_solution(2635277519959119440)
XLA Ops:
  0.6 1.3 slice.33
  1.9 0.7 add_compare_fusion
  2.6 0.7 iota_compare_fusion.5
  3.2 0.7 add_select_fusion
  4.0 1.2 reduce-window.6
  5.5 0.7 compare_select_fusion.5
  6.1 2.4 scatter_custom_fusion
  8.6 0.7 all_to_all.28
  9.3 7.6 %all-to-all-start = ((s32[16,1,32]{2,1,0:T(1,128)}), s32[16,1,32]{2,1,0:T(1,128)S(1)}, u32[]{:S(2)}, u32[]{:S(2)}) async-start(s32[16,1,32]{2,1,0:T(1,128)} %all_to_all.28), calls=%async_computation | async-start | bytes 16384 | tf_op jit(solution)/shard_map/all_to_all | solution.py:101
  16.8 1.1 bitcast_bitcast_fusion.2
  18.0 5.2 %all-to-all-done = s32[16,1,32]{2,1,0:T(1,128)S(1)} async-done(((s32[16,1,32]{2,1,0:T(1,128)}), s32[16,1,32]{2,1,0:T(1,128)S(1)}, u32[]{:S(2)}, u32[]{:S(2)}) %all-to-all-start) | async-done | bytes 2080 | tf_op jit(solution)/shard_map/all_to_all | solution.py:101
  23.3 2.8 %gather_fusion = bf16[512,16,128]{2,1,0:T(8,128)(2,1)} fusion(bf16[128,16,128]{2,1,0:T(8,128)(2,1)S(1)} %bitcast_bitcast_fusion.2, s32[1024]{0:T(1024)S(1)} %pad_clamp_fusion.4), kind=kCustom, calls=%fused_computation | custom fusion | bytes 4196352 | tf_op jit(solution)/shard_map/jit(_take)/gather | solution.py:100
  26.1 2.9 %broadcast_select_fusion = bf16[16,32,16,128]{3,2,1,0:T(8,128)(2,1)} fusion(bf16[16,32,16,128]{3,2,1,0:T(8,128)(2,1)} %bitcast.99, pred[16,32]{1,0:T(8,128)(4,1)S(1)} %compare_and_fusion.1), kind=kLoop, calls=%fused_computation.18 | loop fusion | flops 1048576 | bytes 4194816 | tf_op jit(solution)/shard_map/jit(_take)/select_n | solution.py:100
  29.0 3.8 %all-to-all-start.1 = ((bf16[16,32,16,128]{3,2,1,0:T(8,128)(2,1)}), bf16[16,32,16,128]{3,2,1,0:T(8,128)(2,1)S(1)}, u32[]{:S(2)}, u32[]{:S(2)}) async-start(bf16[16,32,16,128]{3,2,1,0:T(8,128)(2,1)} %broadcast_select_fusion), calls=%async_computation.1 | async-start | bytes 4194304 | tf_op jit(solution)/shard_map/all_to_all | solution.py:103
  32.9 4.5 %copy.78 = bf16[16,16384]{0,1:T(8,128)(2,1)} copy(bf16[16,16384]{1,0:T(8,128)(2,1)} %param.13) | data formatting | bytes 1048576 | tf_op args[0]
  37.4 17.0 %gather_fusion.2 = bf16[4096,16]{1,0:T(8,128)(2,1)} fusion(bf16[16,16384]{0,1:T(8,128)(2,1)} %copy.78, s32[4096]{0:T(1024)S(1)} %fusion.19), kind=kCustom, calls=%fused_computation.2 | custom fusion | bytes 278528 | tf_op jit(solution)/shard_map/jit(_take)/gather | solution.py:60
  54.4 0.7 compare_and_fusion.6
  55.2 0.7 compare_select_fusion.4
  55.9 4.0 %all-to-all-done.1 = bf16[16,32,16,128]{3,2,1,0:T(8,128)(2,1)S(1)} async-done(((bf16[16,32,16,128]{3,2,1,0:T(8,128)(2,1)}), bf16[16,32,16,128]{3,2,1,0:T(8,128)(2,1)S(1)}, u32[]{:S(2)}, u32[]{:S(2)}) %all-to-all-start.1) | async-done | bytes 2097184 | tf_op jit(solution)/shard_map/all_to_all | solution.py:103
  59.9 1.3 copy-done.3
  61.3 2.8 %gather_fusion.1 = bf16[512,16,128]{2,1,0:T(8,128)(2,1)S(1)} fusion(bf16[512,16,128]{2,1,0:T(8,128)(2,1)} %bitcast.97, s32[1024]{0:T(1024)S(1)} %pad_clamp_fusion.3), kind=kCustom, calls=%fused_computation.1 | custom fusion | bytes 4196352 | tf_op jit(solution)/shard_map/jit(_take)/gather | solution.py:105
  64.1 13.7 %fusion = f32[512,16,128]{2,1,0:T(8,128)} fusion(bf16[512,128,128]{2,1,0:T(8,128)(2,1)} %param.14, bf16[512,16,128]{2,1,0:T(8,128)(2,1)S(1)} %gather_fusion.1, pred[512]{0:T(512)(128)(4,1)S(1)} %get-tuple-element.18), kind=kOutput, calls=%fused_computation.15 | convolution fusion | flops 269484032 | bytes 23069184 | tf_op jit(solution)/shard_map/sij,svj->svi/dot_general | solution.py:106
  78.0 41.4 %scatter_fusion = f32[257,16,128]{2,1,0:T(8,128)S(1)} fusion(f32[257,16,128]{2,1,0:T(8,128)S(1)} %broadcast_in_dim.127, s32[512]{0:T(512)S(1)} %bitcast.110, f32[512,16,128]{2,1,0:T(8,128)} %fusion), kind=kCustom, calls=%fused_computation.8 | custom fusion | flops 1048576 | bytes 12584960 | tf_op jit(solution)/shard_map/scatter-add | solution.py:43
  119.5 1.3 copy-done.1
  121.5 4.5 %bitcast_add_fusion = f32[16,4096]{0,1:T(8,128)} fusion(f32[16,4096]{0,1:T(8,128)S(1)} %copy.103, bf16[4096,16]{1,0:T(8,128)(2,1)} %gather_fusion.2, pred[4096]{0:T(1024)(128)(4,1)S(1)} %compare_and_fusion), kind=kLoop, calls=%fused_computation.14 | loop fusion | flops 196608 | bytes 659456 | tf_op jit(solution)/shard_map/add | solution.py:63
  126.0 2.3 copy.79
  128.3 1.5 copy.122
  129.8 9.8 %all-to-all-start.2 = ((f32[8,16,4096]{2,1,0:T(8,128)}), f32[8,16,4096]{2,1,0:T(8,128)S(1)}, u32[]{:S(2)}, u32[]{:S(2)}) async-start(f32[8,16,4096]{2,1,0:T(8,128)} %bitcast.98), calls=%async_computation.2 | async-start | bytes 4194304 | tf_op jit(solution)/shard_map/all_to_all | solution.py:14
  139.8 26.0 %all-to-all-done.2 = f32[8,16,4096]{2,1,0:T(8,128)S(1)} async-done(((f32[8,16,4096]{2,1,0:T(8,128)}), f32[8,16,4096]{2,1,0:T(8,128)S(1)}, u32[]{:S(2)}, u32[]{:S(2)}) %all-to-all-start.2) | async-done | bytes 2097184 | tf_op jit(solution)/shard_map/all_to_all | solution.py:14
  166.8 1.1 broadcast_in_dim.142
  167.9 4.4 %all-to-all-start.3 = ((bf16[8,16,4096]{2,1,0:T(8,128)(2,1)}), bf16[8,16,4096]{2,1,0:T(8,128)(2,1)S(1)}, u32[]{:S(2)}, u32[]{:S(2)}) async-start(bf16[8,16,4096]{2,1,0:T(8,128)(2,1)} %broadcast_in_dim.142), calls=%async_computation.3 | async-start | bytes 2097152 | tf_op jit(solution)/shard_map/all_to_all | solution.py:26
  172.8 1.2 compare_select_fusion.9
  175.2 3.2 %gather_fusion.4 = bf16[1024,16]{1,0:T(8,128)(2,1)S(1)} fusion(bf16[16,4096]{0,1:T(8,128)(2,1)S(1)} %copy.82, s32[1024]{0:T(1024)S(1)} %fusion.20), kind=kCustom, calls=%fused_computation.4 | custom fusion | bytes 69632 | tf_op jit(solution)/shard_map/jit(_take)/gather | solution.py:60
  178.4 8.9 %all-to-all-done.3 = bf16[8,16,4096]{2,1,0:T(8,128)(2,1)S(1)} async-done(((bf16[8,16,4096]{2,1,0:T(8,128)(2,1)}), bf16[8,16,4096]{2,1,0:T(8,128)(2,1)S(1)}, u32[]{:S(2)}, u32[]{:S(2)}) %all-to-all-start.3) | async-done | bytes 1048608 | tf_op jit(solution)/shard_map/all_to_all | solution.py:26
  188.4 1.7 copy.85
  190.1 2.1 gather_fusion.3
  192.2 9.3 %fusion.3 = f32[256,16,128]{2,1,0:T(8,128)} fusion(bf16[256,128,128]{2,1,0:T(8,128)(2,1)} %param.18, bf16[256,16,128]{2,1,0:T(8,128)(2,1)S(1)} %gather_fusion.3, pred[256]{0:T(512)(128)(4,1)S(1)} %copy-done.13), kind=kOutput, calls=%fused_computation.22 | convolution fusion | flops 134742016 | bytes 11534592 | tf_op jit(solution)/shard_map/sij,vsj->svi/dot_general | solution.py:55
  201.5 20.7 %scatter_fusion.1 = f32[129,16,128]{2,1,0:T(8,128)S(1)} fusion(f32[129,16,128]{2,1,0:T(8,128)S(1)} %broadcast_in_dim.139, s32[256]{0:T(256)S(1)} %bitcast.111, f32[256,16,128]{2,1,0:T(8,128)} %fusion.3), kind=kCustom, calls=%fused_computation.9 | custom fusion | flops 524288 | bytes 6292480 | tf_op jit(solution)/shard_map/scatter-add | solution.py:43
  223.4 1.1 copy.123
  224.5 3.7 %all-to-all-start.4 = ((f32[16,16,1024]{2,1,0:T(8,128)}), f32[16,16,1024]{2,1,0:T(8,128)S(1)}, u32[]{:S(2)}, u32[]{:S(2)}) async-start(f32[16,16,1024]{2,1,0:T(8,128)} %bitcast.102), calls=%async_computation.4 | async-start | bytes 2097152 | tf_op jit(solution)/shard_map/all_to_all | solution.py:14
  228.3 15.7 %all-to-all-done.4 = f32[16,16,1024]{2,1,0:T(8,128)S(1)} async-done(((f32[16,16,1024]{2,1,0:T(8,128)}), f32[16,16,1024]{2,1,0:T(8,128)S(1)}, u32[]{:S(2)}, u32[]{:S(2)}) %all-to-all-start.4) | async-done | bytes 1048608 | tf_op jit(solution)/shard_map/all_to_all | solution.py:14
  244.4 0.9 broadcast_in_dim.151
  245.3 4.2 %all-to-all-start.5 = ((bf16[16,16,1024]{2,1,0:T(8,128)(2,1)}), bf16[16,16,1024]{2,1,0:T(8,128)(2,1)S(1)}, u32[]{:S(2)}, u32[]{:S(2)}) async-start(bf16[16,16,1024]{2,1,0:T(8,128)(2,1)} %broadcast_in_dim.151), calls=%async_computation.5 | async-start | bytes 1048576 | tf_op jit(solution)/shard_map/all_to_all | solution.py:26
  250.7 0.9 gather_fusion.6
  251.6 7.7 %all-to-all-done.5 = bf16[16,16,1024]{2,1,0:T(8,128)(2,1)S(1)} async-done(((bf16[16,16,1024]{2,1,0:T(8,128)(2,1)}), bf16[16,16,1024]{2,1,0:T(8,128)(2,1)S(1)}, u32[]{:S(2)}, u32[]{:S(2)}) %all-to-all-start.5) | async-done | bytes 524320 | tf_op jit(solution)/shard_map/all_to_all | solution.py:26
  260.7 0.7 fusion.9
  261.5 1.7 scatter_fusion.2
  263.6 10.4 %all_to_all.45 = f32[8,16,256]{2,1,0:T(8,128)S(1)} all-to-all(f32[8,16,256]{2,1,0:T(8,128)S(1)} %bitcast.105), channel_id=1, replica_groups=mesh['row'=8,'col'=16] {'row'}, dimensions={0} | all-to-all | bytes 262144 | tf_op jit(solution)/shard_map/all_to_all | solution.py:14
  (98 shorter events, 10.9 us)
Async XLA Ops:
  0.6 260.1 %copy-start = (bf16[32,128,128]{2,1,0:T(8,128)(2,1)S(1)}, bf16[32,128,128]{2,1,0:T(8,128)(2,1)}, u32[]{:S(2)}) copy-start(bf16[32,128,128]{2,1,0:T(8,128)(2,1)} %param.22) | copy-start | bytes 3145732
  9.3 13.9 %all-to-all-start = ((s32[16,1,32]{2,1,0:T(1,128)}), s32[16,1,32]{2,1,0:T(1,128)S(1)}, u32[]{:S(2)}, u32[]{:S(2)}) async-start(s32[16,1,32]{2,1,0:T(1,128)} %all_to_all.28), calls=%async_computation | async-start | bytes 16384 | tf_op jit(solution)/shard_map/all_to_all | solution.py:101
  29.0 3.9 %copy-start.14 = (s32[257]{0:T(512)S(1)}, s32[257]{0:T(512)}, u32[]{:S(2)}) copy-start(s32[257]{0:T(512)} %param.15) | copy-start | bytes 3088
  29.0 30.9 %all-to-all-start.1 = ((bf16[16,32,16,128]{3,2,1,0:T(8,128)(2,1)}), bf16[16,32,16,128]{3,2,1,0:T(8,128)(2,1)S(1)}, u32[]{:S(2)}, u32[]{:S(2)}) async-start(bf16[16,32,16,128]{3,2,1,0:T(8,128)(2,1)} %broadcast_select_fusion), calls=%async_computation.1 | async-start | bytes 4194304 | tf_op jit(solution)/shard_map/all_to_all | solution.py:103
  32.9 4.5 %copy-start.6 = (s32[4096]{0:T(1024)S(1)}, s32[4096]{0:T(1024)}, u32[]{:S(2)}) copy-start(s32[4096]{0:T(1024)} %param.17) | copy-start | bytes 49156
  59.9 1.4 copy-start.3
  119.5 1.4 copy-start.1
  126.0 2.3 copy-start.2
  129.8 9.8 %copy-start.15 = (s32[129]{0:T(256)S(1)}, s32[129]{0:T(256)}, u32[]{:S(2)}) copy-start(s32[129]{0:T(256)} %param.19) | copy-start | bytes 1552
  129.8 10.0 %copy-start.8 = (s32[256]{0:T(256)S(1)}, s32[256]{0:T(256)}, u32[]{:S(2)}) copy-start(s32[256]{0:T(256)} %param.20) | copy-start | bytes 3076
  129.8 36.0 %all-to-all-start.2 = ((f32[8,16,4096]{2,1,0:T(8,128)}), f32[8,16,4096]{2,1,0:T(8,128)S(1)}, u32[]{:S(2)}, u32[]{:S(2)}) async-start(f32[8,16,4096]{2,1,0:T(8,128)} %bitcast.98), calls=%async_computation.2 | async-start | bytes 4194304 | tf_op jit(solution)/shard_map/all_to_all | solution.py:14
  166.4 7.6 %copy-start.9 = (s32[256]{0:T(256)S(1)}, s32[256]{0:T(256)}, u32[]{:S(2)}) copy-start(s32[256]{0:T(256)} %param.25) | copy-start | bytes 3076
  166.4 8.2 %copy-start.7 = (s32[1024]{0:T(1024)S(1)}, s32[1024]{0:T(1024)}, u32[]{:S(2)}) copy-start(s32[1024]{0:T(1024)} %param.21) | copy-start | bytes 12292
  166.8 21.1 %copy-start.4 = (bf16[16,4096]{1,0:T(8,128)(2,1)}, bf16[16,4096]{1,0:T(8,128)(2,1)S(1)}, u32[]{:S(2)}) copy-start(bf16[16,4096]{1,0:T(8,128)(2,1)S(1)} %copy.99) | copy-start | bytes 393220
  167.9 19.4 %all-to-all-start.3 = ((bf16[8,16,4096]{2,1,0:T(8,128)(2,1)}), bf16[8,16,4096]{2,1,0:T(8,128)(2,1)S(1)}, u32[]{:S(2)}, u32[]{:S(2)}) async-start(bf16[8,16,4096]{2,1,0:T(8,128)(2,1)} %broadcast_in_dim.142), calls=%async_computation.3 | async-start | bytes 2097152 | tf_op jit(solution)/shard_map/all_to_all | solution.py:26
  188.4 3.8 %copy-start.13 = (pred[256]{0:T(512)(128)(4,1)S(1)}, pred[256]{0:T(512)(128)(4,1)}, u32[]{:S(2)}) copy-start(pred[256]{0:T(512)(128)(4,1)} %get-tuple-element.23) | copy-start | bytes 772
  192.2 9.3 %copy-start.11 = (s32[256,1]{0,1:T(1,128)S(1)}, s32[256,1]{0,1:T(1,128)}, u32[]{:S(2)}) copy-start(s32[256,1]{0,1:T(1,128)} %compare_select_fusion.9) | copy-start | bytes 3076
  222.3 0.7 copy-start.10
  223.4 4.8 %copy-start.16 = (s32[17]{0:T(128)S(1)}, s32[17]{0:T(128)}, u32[]{:S(2)}) copy-start(s32[17]{0:T(128)} %param.23) | copy-start | bytes 208
  223.4 4.8 %copy-start.17 = (s32[32]{0:T(128)S(1)}, s32[32]{0:T(128)}, u32[]{:S(2)}) copy-start(s32[32]{0:T(128)} %param.24) | copy-start | bytes 388
  224.5 19.6 %all-to-all-start.4 = ((f32[16,16,1024]{2,1,0:T(8,128)}), f32[16,16,1024]{2,1,0:T(8,128)S(1)}, u32[]{:S(2)}, u32[]{:S(2)}) async-start(f32[16,16,1024]{2,1,0:T(8,128)} %bitcast.102), calls=%async_computation.4 | async-start | bytes 2097152 | tf_op jit(solution)/shard_map/all_to_all | solution.py:14
  244.4 15.7 %copy-start.5 = (bf16[16,1024]{1,0:T(8,128)(2,1)}, bf16[16,1024]{1,0:T(8,128)(2,1)S(1)}, u32[]{:S(2)}) copy-start(bf16[16,1024]{1,0:T(8,128)(2,1)S(1)} %copy.100) | copy-start | bytes 98308
  245.3 14.0 %all-to-all-start.5 = ((bf16[16,16,1024]{2,1,0:T(8,128)(2,1)}), bf16[16,16,1024]{2,1,0:T(8,128)(2,1)S(1)}, u32[]{:S(2)}, u32[]{:S(2)}) async-start(bf16[16,16,1024]{2,1,0:T(8,128)(2,1)} %broadcast_in_dim.151), calls=%async_computation.5 | async-start | bytes 1048576 | tf_op jit(solution)/shard_map/all_to_all | solution.py:26
  259.8 3.6 %copy-start.12 = (pred[256]{0:T(512)(128)(4,1)S(1)}, pred[256]{0:T(512)(128)(4,1)}, u32[]{:S(2)}) copy-start(pred[256]{0:T(512)(128)(4,1)} %get-tuple-element.22) | copy-start | bytes 772
where the time goes:
time: 276 us; the launch traced here: 275 us
  other arithmetic  81.1 us (29%)
  waiting for transfers between devices  67.5 us (24%)
  local copies, waits for them, and re-layouts  57.2 us (21%)
  starting transfers between devices  33.5 us (12%)
  matrix products  23.7 us (9%)
  blocking collectives  10.4 us (4%)
    scatter-add x3, other arithmetic, block_sums(): jax.ops.segment_sum(products, segment, num_segments=block_count + 1, indi...  63.9 us
    all_to_all x2, waiting for transfers between devices, summed_on_arrival(): lax.all_to_all(parts, axis, split_axis=0, concat_axis=0, tiled=True)  41.7 us
    gather x3, local copies, waits for them, and re-layouts, add_points(): injected = jnp.take(own_piece, points, axis=1).astype(jnp.float32)  21 us
    all_to_all x2, waiting for transfers between devices, from_everyone(): return lax.all_to_all(copies, axis, split_axis=0, concat_axis=0, tiled=True)  16.5 us
    dot_general x1, matrix products, on_device(): jnp.einsum('sij,svj->svi', tiles_one, picked, preferred_element_type=jnp....  13.7 us
    all_to_all x2, starting transfers between devices, summed_on_arrival(): lax.all_to_all(parts, axis, split_axis=0, concat_axis=0, tiled=True)  13.5 us
    all_to_all x1, blocking collectives, summed_on_arrival(): lax.all_to_all(parts, axis, split_axis=0, concat_axis=0, tiled=True)  10.4 us
    dot_general x2, matrix products, group_products(): jnp.einsum('sij,vsj->svi', tiles, picked, preferred_element_type=jnp.floa...  9.93 us
  transfers between devices with their start and end apart: 6, of which 6 were waited for; matrix products, arithmetic and copies ran while one was open for 12% of the time, Pallas kernels for 0%

commit v1 on v0

v1 whole, which is shorter than its diff:
```python
import jax
import jax.numpy as jnp
from jax import lax
from jax.experimental import pallas as pl
from jax.experimental.pallas import tpu as pltpu
from jax.sharding import PartitionSpec as P

MESH = pl.DeviceIdType.MESH
F32 = jnp.float32
BF16 = jnp.bfloat16
I32 = jnp.int32
E = 128
V = 16
ORDER = (
    (1, 1), (3, 3), (0, 2), (1, 3), (3, 1), (2, 0), (1, 2), (3, 2),
    (2, 1), (2, 3), (0, 1), (0, 3), (1, 0), (3, 0), (2, 2),
)
NT = (((1,), (1,)), ((), ()))


def inject(load, n_src, points, first, group, store):
    low, high = [], []
    for i in range(group):
        row = jnp.broadcast_to(points[pl.ds(first + i, 1), :], (V, E))
        low.append(row & (E - 1))
        high.append(row >> 7)

    def source(j, held):
        block = load(j).astype(F32)
        return tuple(
            jnp.where(
                high[i] == j,
                jnp.take_along_axis(block, low[i], axis=1, mode="promise_in_bounds"),
                held[i],
            )
            for i in range(group)
        )

    zero = jnp.zeros((V, E), F32)
    held = lax.fori_loop(0, n_src, source, (zero,) * group, unroll=8)
    for i in range(group):
        store(i, held[i])


def plan(ptr1, cols1, ask, slot, tgt):
    n1 = cols1.shape[1]
    live = ptr1[ptr1.shape[0] - 1]
    names = cols1[...]
    lanes = lax.broadcasted_iota(I32, (1, n1), 1)
    owner = names >> 7
    hit = jnp.where(
        (lax.broadcasted_iota(I32, (16, n1), 0) == owner) & (lanes < live), 1.0, 0.0
    ).astype(F32)
    before = jnp.where(
        lax.broadcasted_iota(I32, (n1, n1), 0) < lax.broadcasted_iota(I32, (n1, n1), 1), 1.0, 0.0
    ).astype(BF16)
    count = jnp.dot(hit.astype(BF16), before, preferred_element_type=F32)
    rank = jnp.sum(hit * count, axis=0, keepdims=True)
    tgt[...] = jnp.where(lanes < live, owner * 32 + rank.astype(I32), 0)
    place = jnp.where(
        lax.broadcasted_iota(I32, (E, n1), 0).astype(F32) == rank, 1.0, 0.0
    ).astype(BF16)
    listed = jnp.concatenate(
        [
            hit * (names & (E - 1)).astype(F32),
            hit * (lanes >> 8).astype(F32),
            hit * (lanes & 255).astype(F32),
        ],
        axis=0,
    ).astype(BF16)
    table = lax.dot_general(listed, place, NT, preferred_element_type=F32).astype(I32)
    for p in range(16):
        ask[p] = table[p : p + 1]
        slot[p] = table[16 + p : 17 + p] * 256 + table[32 + p : 33 + p]


def kernel(
    ask, pts1, pts2, pts3, s_tgt, s_slot, ptr1, cols2, ptr2, cols3, ptr3,
    fine_hbm, t1_hbm, t2_hbm, t3_hbm,
    out1_hbm, out2_hbm, out3_hbm,
    fine, blocks, t1, t2, t3,
    asked, s_asked,
    snd, got, prod, run,
    d_snd, d_got, own1, z_snd, z_got, inj1, g1,
    c_snd, c_got, own2, inj2, g2,
    r_snd, r_got, out1, out2, out3,
    ld_sem, t_sem, ix_sem,
    ask_s, ask_r, rep_s, rep_r, d_s, d_r, z_s, z_r, a_s, a_r,
    p_s, p_r, q_s, q_r, m_s, m_r, o_sem,
):
    row = lax.axis_index("row")
    col = lax.axis_index("col")
    z, core = row // 2, lax.rem(row, 2)
    y, x = col // 4, lax.rem(col, 4)
    other = 1 - core

    def at(dx, dy):
        return lax.rem(y + dy, 4) * 4 + lax.rem(x + dx, 4)

    def remote(src, dst, send, recv, **device):
        return pltpu.make_async_remote_copy(
            src_ref=src, dst_ref=dst, send_sem=send, recv_sem=recv,
            device_id=device, device_id_type=MESH,
        )

    load_fine = pltpu.make_async_copy(fine_hbm, fine, ld_sem.at[0])
    load_fine.start()
    load_t1 = pltpu.make_async_copy(t1_hbm, t1, t_sem.at[0])
    load_t1.start()
    load_t2 = pltpu.make_async_copy(t2_hbm, t2, t_sem.at[1])
    load_t3 = pltpu.make_async_copy(t3_hbm, t3, t_sem.at[2])

    barrier = pltpu.get_barrier_semaphore()
    for d in range(1, 16):
        pl.semaphore_signal(barrier, inc=1, device_id={"col": lax.rem(col + d, 16)}, device_id_type=MESH)
    for d in range(1, 8):
        pl.semaphore_signal(barrier, inc=1, device_id={"row": lax.rem(row + d, 8)}, device_id_type=MESH)

    pl.semaphore_wait(barrier, 22)

    asks = []
    for dx, dy in ORDER:
        peer = at(dx, dy)
        copy = remote(ask.at[peer], asked.at[col], ask_s.at[peer], ask_r.at[col], col=peer)
        copy.start()
        asks.append(copy)
    asked[col] = ask[col]
    load_fine.wait()

    def cut(j, carry):
        blocks[j] = fine[:, pl.ds(pl.multiple_of(j * E, E), E)]
        return carry

    lax.fori_loop(0, 128, cut, 0, unroll=8)
    for dx, dy in ORDER:
        peer = at(dx, dy)
        remote(ask.at[peer], asked.at[peer], ask_s.at[peer], ask_r.at[peer], col=peer).wait_recv()
    copy_asked = pltpu.make_async_copy(asked, s_asked, ix_sem.at[0])
    copy_asked.start()
    copy_asked.wait()

    replies = []

    def pick(peer, k):
        return blocks[s_asked[peer, 0, k]]

    for half in range(2):
        for dx, dy in ORDER:
            peer = at(dx, dy)

            def fill(k, carry, peer=peer):
                snd[peer, k] = pick(peer, k)
                return carry

            lax.fori_loop(half * 16, half * 16 + 16, fill, 0, unroll=8)
            part = pl.ds(half * 16, 16)
            copy = remote(
                snd.at[peer, part], got.at[col, part], rep_s.at[peer, half], rep_r.at[col, half], col=peer
            )
            copy.start()
            replies.append(copy)

    def fill_own(k, carry):
        got[col, k] = pick(col, k)
        return carry

    lax.fori_loop(0, 32, fill_own, 0, unroll=8)
    load_t2.start()
    load_t3.start()

    def inject_one(g, carry):
        def store(i, block):
            inj1[g * 8 + i] = block.astype(BF16)

        inject(lambda j: blocks[j], 128, pts1, g * 8, 8, store)
        return carry

    lax.fori_loop(0, 4, inject_one, 0)
    load_t1.wait()

    def products(peer, half):
        def one(k, carry):
            w = t1[s_slot[peer, 0, k]]
            prod[peer * 32 + k] = lax.dot_general(got[peer, k], w, NT, preferred_element_type=F32)
            return carry

        lax.fori_loop(half * 16, half * 16 + 16, one, 0, unroll=8)

    for half in range(2):
        products(col, half)
        for dx, dy in ORDER:
            peer = at(4 - dx, 4 - dy)
            part = pl.ds(half * 16, 16)
            remote(
                snd.at[peer, part], got.at[peer, part], rep_s.at[peer, half], rep_r.at[peer, half], col=peer
            ).wait_recv()
            products(peer, half)

    zero = jnp.zeros((V, E), F32)
    run[0] = zero

    def add_one(s, total):
        total = total + prod[s_tgt[0, s]]
        run[s + 1] = total
        return total

    lax.fori_loop(0, t1.shape[0], add_one, zero, unroll=8)

    def sums(ptr, b):
        return run[ptr[b + 1]] - run[ptr[b]]

    for dz in (1, 3, 2, 0):
        zt = lax.rem(z + dz, 4)

        def give(i, carry, zt=zt):
            d_snd[zt, i] = sums(ptr1, zt * 64 + other * 32 + i).astype(BF16)
            return carry

        lax.fori_loop(0, 32, give, 0, unroll=8)
        remote(d_snd.at[zt], d_got.at[zt], d_s.at[zt], d_r.at[zt], row=z * 2 + other).start()
    for dz in (1, 3, 2, 0):
        zt = lax.rem(z + dz, 4)

        def keep(i, carry, zt=zt):
            own1[zt, i] = sums(ptr1, zt * 64 + core * 32 + i)
            return carry

        lax.fori_loop(0, 32, keep, 0, unroll=8)
    for dz in (1, 3, 2):
        zt = lax.rem(z + dz, 4)
        remote(d_snd.at[zt], d_got.at[zt], d_s.at[zt], d_r.at[zt], row=z * 2 + other).wait_recv()

        def join(i, carry, zt=zt):
            z_snd[zt, i] = (own1[zt, i] + d_got[zt, i].astype(F32)).astype(BF16)
            return carry

        lax.fori_loop(0, 32, join, 0, unroll=8)
        remote(z_snd.at[zt], z_got.at[z], z_s.at[zt], z_r.at[z], row=zt * 2 + core).start()
    remote(d_snd.at[z], d_got.at[z], d_s.at[z], d_r.at[z], row=z * 2 + other).wait_recv()

    def base(i, carry):
        own1[z, i] = own1[z, i] + d_got[z, i].astype(F32) + inj1[i].astype(F32)
        return carry

    lax.fori_loop(0, 32, base, 0, unroll=8)
    for dz in (1, 3, 2):
        zt = lax.rem(z + dz, 4)
        remote(z_snd.at[zt], z_got.at[zt], z_s.at[zt], z_r.at[zt], row=zt * 2 + core).wait_recv()
    za, zb, zc = lax.rem(z + 1, 4), lax.rem(z + 3, 4), lax.rem(z + 2, 4)

    def final_one(i, carry):
        total = own1[z, i] + (
            (z_got[za, i].astype(F32) + z_got[zb, i].astype(F32)) + z_got[zc, i].astype(F32)
        )
        block = total.astype(BF16)
        g1[row * 32 + i] = block
        out1[:, pl.ds(pl.multiple_of(i * E, E), E)] = block
        return carry

    lax.fori_loop(0, 32, final_one, 0, unroll=8)

    def piece(r):
        return g1.at[pl.ds(r * 32, 32)]

    for dz in (1, 3, 2):
        zt = lax.rem(z + dz, 4)
        remote(piece(row), piece(row), a_s.at[zt, 0], a_r.at[row], row=zt * 2 + core).start()
    remote(piece(row), piece(row), a_s.at[z, 1], a_r.at[row], row=z * 2 + other).start()
    write1 = pltpu.make_async_copy(out1, out1_hbm, o_sem.at[0])
    write1.start()

    def store2(i, block):
        inj2[i] = block

    inject(lambda j: g1[row * 32 + j], 32, pts2, 0, 8, store2)
    load_t2.wait()
    for dz in (1, 3, 2):
        zt = lax.rem(z + dz, 4)
        r = zt * 2 + core
        remote(piece(r), piece(r), a_s.at[zt, 0], a_r.at[r], row=r).wait_recv()
        remote(piece(r), piece(r), a_s.at[zt, 1], a_r.at[r], row=z * 2 + other).start()
    for dz in (0, 1, 3, 2):
        zt = lax.rem(z + dz, 4)
        r = zt * 2 + other
        remote(piece(r), piece(r), a_s.at[zt, 1], a_r.at[r], row=z * 2 + other).wait_recv()

    def slot_two(s, total):
        w = t2[s]
        total = total + lax.dot_general(g1[cols2[s]], w, NT, preferred_element_type=F32)
        run[s + 1] = total
        return total

    lax.fori_loop(0, t2.shape[0], slot_two, zero, unroll=8)
    for dx, dy in ORDER:
        peer = at(dx, dy)

        def give2(i, carry, peer=peer):
            c_snd[peer, i] = sums(ptr2, peer * 8 + i).astype(BF16)
            return carry

        lax.fori_loop(0, 8, give2, 0, unroll=8)
        remote(c_snd.at[peer], c_got.at[col], p_s.at[peer], p_r.at[col], col=peer).start()

    for i in range(8):
        own2[i] = sums(ptr2, col * 8 + i) + inj2[i]
    for dx, dy in ORDER:
        peer = at(4 - dx, 4 - dy)
        remote(c_snd.at[peer], c_got.at[peer], p_s.at[peer], p_r.at[peer], col=peer).wait_recv()

    def final_two(i, carry):
        total = own2[i]
        for dx, dy in ORDER:
            total = total + c_got[at(dx, dy), i].astype(F32)
        block = total.astype(BF16)
        g2[col * 8 + i] = block
        out2[:, pl.ds(pl.multiple_of(i * E, E), E)] = block
        return carry

    lax.fori_loop(0, 8, final_two, 0)

    def piece2(c):
        return g2.at[pl.ds(c * 8, 8)]

    for dx, dy in ORDER:
        peer = at(dx, dy)
        remote(piece2(col), piece2(col), q_s.at[peer], q_r.at[col], col=peer).start()
    write2 = pltpu.make_async_copy(out2, out2_hbm, o_sem.at[1])
    write2.start()

    held = []

    def store3(i, block):
        held.append(block)

    inject(lambda j: g2[col * 8 + j], 8, pts3, 0, 2, store3)
    load_t3.wait()
    for dx, dy in ORDER:
        peer = at(4 - dx, 4 - dy)
        remote(piece2(peer), piece2(peer), q_s.at[peer], q_r.at[peer], col=peer).wait_recv()

    def slot_three(s, total):
        w = t3[s]
        total = total + lax.dot_general(g2[cols3[s]], w, NT, preferred_element_type=F32)
        run[s + 1] = total
        return total

    lax.fori_loop(0, t3.shape[0], slot_three, zero, unroll=8)
    for d in range(1, 8):
        peer = lax.rem(row + d, 8)
        for i in range(2):
            r_snd[peer, i] = sums(ptr3, peer * 2 + i).astype(BF16)
        remote(r_snd.at[peer], r_got.at[row], m_s.at[peer], m_r.at[row], row=peer).start()
    held = [held[i] + sums(ptr3, row * 2 + i) for i in range(2)]
    for d in range(1, 8):
        peer = lax.rem(row + d, 8)
        remote(r_snd.at[peer], r_got.at[peer], m_s.at[peer], m_r.at[peer], row=peer).wait_recv()
        held = [held[i] + r_got[peer, i].astype(F32) for i in range(2)]
    for i in range(2):
        out3[:, i * E : (i + 1) * E] = held[i].astype(BF16)
    write3 = pltpu.make_async_copy(out3, out3_hbm, o_sem.at[2])
    write3.start()

    for copy in asks:
        copy.wait_send()
    for copy in replies:
        copy.wait_send()
    for zt in range(4):
        remote(d_snd.at[zt], d_got.at[zt], d_s.at[zt], d_r.at[zt], row=z * 2 + other).wait_send()
    for dz in (1, 2, 3):
        zt = lax.rem(z + dz, 4)
        r = zt * 2 + core
        remote(z_snd.at[zt], z_got.at[z], z_s.at[zt], z_r.at[z], row=r).wait_send()
        remote(piece(row), piece(row), a_s.at[zt, 0], a_r.at[row], row=r).wait_send()
    for zt in range(4):
        r = zt * 2 + core
        remote(piece(r), piece(r), a_s.at[zt, 1], a_r.at[r], row=z * 2 + other).wait_send()
    for dx, dy in ORDER:
        peer = at(dx, dy)
        remote(c_snd.at[peer], c_got.at[col], p_s.at[peer], p_r.at[col], col=peer).wait_send()
        remote(piece2(col), piece2(col), q_s.at[peer], q_r.at[col], col=peer).wait_send()
    for d in range(1, 8):
        peer = lax.rem(row + d, 8)
        remote(r_snd.at[peer], r_got.at[row], m_s.at[peer], m_r.at[row], row=peer).wait_send()
    write1.wait()
    write2.wait()
    write3.wait()


def on_device(
    fine, tiles1, ptr1, cols1, pts1, tiles2, ptr2, cols2, pts2, tiles3, ptr3, cols3, pts3
):
    n1, n2, n3 = tiles1.shape[0], tiles2.shape[0], tiles3.shape[0]
    hbm = pl.BlockSpec(memory_space=pl.ANY)
    vmem = pl.BlockSpec(memory_space=pltpu.VMEM)
    smem = pl.BlockSpec(memory_space=pltpu.SMEM)
    dma = pltpu.SemaphoreType.DMA
    outs = [
        jax.ShapeDtypeStruct((V, pts1.shape[0]), BF16),
        jax.ShapeDtypeStruct((V, pts2.shape[0]), BF16),
        jax.ShapeDtypeStruct((V, pts3.shape[0]), BF16),
    ]
    vm = pltpu.VMEM
    scratch = [
        vm(fine.shape, BF16), vm((128, V, E), BF16), vm(tiles1.shape, BF16), vm(tiles2.shape, BF16), vm(tiles3.shape, BF16),
        vm((16, 1, E), I32), pltpu.SMEM((16, 1, E), I32),
        vm((16, 32, V, E), BF16), vm((16, 32, V, E), BF16), vm((n1, V, E), F32), vm((n1 + 1, V, E), F32),
        vm((4, 32, V, E), BF16), vm((4, 32, V, E), BF16), vm((4, 32, V, E), F32),
        vm((4, 32, V, E), BF16), vm((4, 32, V, E), BF16), vm((32, V, E), BF16), vm((256, V, E), BF16),
        vm((16, 8, V, E), BF16), vm((16, 8, V, E), BF16), vm((8, V, E), F32), vm((8, V, E), F32), vm((128, V, E), BF16),
        vm((8, 2, V, E), BF16), vm((8, 2, V, E), BF16),
        vm(outs[0].shape, BF16), vm(outs[1].shape, BF16), vm(outs[2].shape, BF16),
        dma((1,)), dma((3,)), dma((1,)),
        dma((16,)), dma((16,)), dma((16, 2)), dma((16, 2)), dma((4,)), dma((4,)), dma((4,)), dma((4,)), dma((4, 2)), dma((8,)),
        dma((16,)), dma((16,)), dma((16,)), dma((16,)), dma((8,)), dma((8,)), dma((3,)),
    ]
    ask, slot, tgt = pl.pallas_call(
        plan,
        out_shape=[
            jax.ShapeDtypeStruct((16, 1, E), I32),
            jax.ShapeDtypeStruct((16, 1, E), I32),
            jax.ShapeDtypeStruct((1, n1), I32),
        ],
        in_specs=[smem, vmem],
        out_specs=[vmem] * 3,
        name="plan",
    )(ptr1, cols1.reshape(1, n1))
    return pl.pallas_call(
        kernel,
        out_shape=outs,
        in_specs=[vmem] * 4 + [smem] * 7 + [hbm] * 4,
        out_specs=[hbm] * 3,
        scratch_shapes=scratch,
        compiler_params=pltpu.CompilerParams(
            collective_id=0, has_side_effects=True, vmem_limit_bytes=58 << 20
        ),
        name="restrict",
    )(
        ask, pts1.reshape(-1, E), pts2.reshape(-1, E), pts3.reshape(-1, E),
        tgt, slot, ptr1, cols2, ptr2, cols3, ptr3, fine, tiles1, tiles2, tiles3,
    )


def solution(mesh):
    placed = (
        P(None, ("row", "col")),
        P(("row", "col"), None, None),
        P(("row", "col")),
        P(("row", "col")),
        P(("col", "row")),
        P(("row", "col"), None, None),
        P(("row", "col")),
        P(("row", "col")),
        P(("row", "col")),
        P(("row", "col"), None, None),
        P(("row", "col")),
        P(("row", "col")),
        P(("col", "row")),
    )
    return jax.shard_map(
        on_device,
        mesh=mesh,
        in_specs=placed,
        out_specs=(P(None, ("col", "row")), P(None, ("row", "col")), P(None, ("col", "row"))),
        check_vma=False,
    )
```

time: 276 us -> 109 us (0.39)
  Pallas kernels: 0 us -> 104 us
  other arithmetic: 81.1 us -> 0 us
  waiting for transfers between devices: 67.5 us -> 0 us
  local copies, waits for them, and re-layouts: 57.2 us -> 4.24 us
  starting transfers between devices: 33.5 us -> 0 us
  matrix products: 23.7 us -> 0 us
  blocking collectives: 10.4 us -> 0 us
    pallas_call x0 -> x2, Pallas kernels: none -> 104 us  [the longest x1 102 us: on_device(): pl.pallas_call(kernel, out_shape=outs, in_specs=[vmem] * 4 + [smem] * 7 +...]
    all_to_all x6 -> x0, waiting for transfers between devices: 67.5 us -> none  [the longest x2 41.7 us: summed_on_arrival(): lax.all_to_all(parts, axis, split_axis=0, concat_axis=0, tiled=True)]
    scatter-add x3 -> x0, other arithmetic: 63.9 us -> none  [block_sums(): jax.ops.segment_sum(products, segment, num_segments=block_count + 1, indi...]
    all_to_all x6 -> x0, starting transfers between devices: 33.5 us -> none  [the longest x2 13.5 us: summed_on_arrival(): lax.all_to_all(parts, axis, split_axis=0, concat_axis=0, tiled=True)]
    gather x7 -> x0, local copies, waits for them, and re-layouts: 29.2 us -> none  [the longest x3 21 us: add_points(): injected = jnp.take(own_piece, points, axis=1).astype(jnp.float32)]
    dot_general x3 -> x0, matrix products: 23.7 us -> none  [the longest x1 13.7 us: on_device(): jnp.einsum('sij,svj->svi', tiles_one, picked, preferred_element_type=jnp....]
    all_to_all x1 -> x0, blocking collectives: 10.4 us -> none  [summed_on_arrival(): lax.all_to_all(parts, axis, split_axis=0, concat_axis=0, tiled=True)]
    select_n x10 -> x0, other arithmetic: 6.82 us -> none  [the longest x2 2.94 us: on_device(): jnp.take(own_blocks, lax.all_to_all(requests, 'col', split_axis=0, concat...]
  transfers between devices with their start and end apart: 6 -> 0, of which waited for: 6 -> 0; matrix products, arithmetic and copies ran while one was open for 12% -> 0% of each run, Pallas kernels for 0% -> 0%
where the time goes in v1:
time: 109 us
  Pallas kernels  104 us (95%)
  local copies, waits for them, and re-layouts  4.24 us (4%)
    pallas_call x1, Pallas kernels, on_device(): pl.pallas_call(kernel, out_shape=outs, in_specs=[vmem] * 4 + [smem] * 7 +...  102 us
    unnamed x3, local copies, waits for them, and re-layouts  4.24 us

profile of v1, /device:TPU:1, one launch (start us, length us, event | category | flops | bytes accessed | tf_op | source)
XLA Modules:
  0.0 109.0 jit_solution(13710382431775247225)
XLA Ops:
  0.6 1.7 %plan.1 = (s32[16,1,128]{2,1,0:T(1,128)}, s32[16,1,128]{2,1,0:T(1,128)}, s32[1,512]{1,0:T(1,128)}) custom-call(s32[257]{0:T(512)} %ptr1.3, s32[1,512]{1,0:T(1,128)} %bitcast.6), custom_call_target="tpu_custom_call" | custom-call | tf_op jit(solution)/shard_map/plan/pallas_call | solution.py:416
  2.3 102.5 %restrict.1 = (bf16[16,4096]{1,0:T(8,128)(2,1)}, bf16[16,1024]{1,0:T(8,128)(2,1)}, bf16[16,256]{1,0:T(8,128)(2,1)}) custom-call(s32[16,1,128]{2,1,0:T(1,128)} %get-tuple-element.6.ask, s32[32,128]{1,0:T(8,128)} %bitcast.4, s32[8,128]{1,0:T(8,128)} %bitcast.5, s32[2,128]{1,0:T(2,128)} %bitcast.7, s32[1,512]{1,0:T(1,128)} %get-tuple-element.7.s_tgt, ...), custom_call_target="tpu_custom_call" | custom-call | tf_op jit(solution)/shard_map/restrict/pallas_call | solution.py:427
  104.8 1.6 %copy.19 = bf16[16,4096]{1,0:T(8,128)(2,1)} copy(bf16[16,4096]{1,0:T(8,128)(2,1)} %get-tuple-element.12) | data formatting | bytes 262144
  106.3 1.4 %copy.20 = bf16[16,1024]{1,0:T(8,128)(2,1)} copy(bf16[16,1024]{1,0:T(8,128)(2,1)} %get-tuple-element.13) | data formatting | bytes 65536
  107.7 1.3 %copy.21 = bf16[16,256]{1,0:T(8,128)(2,1)} copy(bf16[16,256]{1,0:T(8,128)(2,1)} %get-tuple-element.14) | data formatting | bytes 16384

commit v2 on v1

v2 whole, which is shorter than its diff:
```python
import jax
import jax.numpy as jnp
from jax import lax
from jax.experimental import pallas as pl
from jax.experimental.pallas import tpu as pltpu
from jax.sharding import PartitionSpec as P

MESH = pl.DeviceIdType.MESH
F32 = jnp.float32
BF16 = jnp.bfloat16
I32 = jnp.int32
E = 128
V = 16
ORDER = (
    (1, 1), (3, 3), (0, 2), (1, 3), (3, 1), (2, 0), (1, 2), (3, 2),
    (2, 1), (2, 3), (0, 1), (0, 3), (1, 0), (3, 0), (2, 2),
)
H = 8
NEG = tuple(ORDER.index(((4 - dx) % 4, (4 - dy) % 4)) for dx, dy in ORDER)
NT = (((1,), (1,)), ((), ()))


def at(col, offset):
    return lax.rem(col // 4 + offset[1], 4) * 4 + lax.rem(lax.rem(col, 4) + offset[0], 4)


def inject(load, n_src, points, first, group, store):
    low, high = [], []
    rows = load(0).shape[0]
    for i in range(group):
        line = jnp.broadcast_to(points[pl.ds(first + i, 1), :], (rows, E))
        low.append(line & (E - 1))
        high.append(line >> 7)

    def source(j, held):
        block = load(j).astype(F32)
        return tuple(
            jnp.where(
                high[i] == j,
                jnp.take_along_axis(block, low[i], axis=1, mode="promise_in_bounds"),
                held[i],
            )
            for i in range(group)
        )

    zero = jnp.zeros((rows, E), F32)
    held = lax.fori_loop(0, n_src, source, (zero,) * group, unroll=8)
    for i in range(group):
        store(i, held[i])


def pair_products(x, other_x, w, other_w):
    none = jnp.zeros_like(x)
    lhs = jnp.concatenate(
        [jnp.concatenate([x, none], axis=1), jnp.concatenate([none, other_x], axis=1)], axis=0
    )
    both = lax.dot_general(
        lhs, jnp.concatenate([w, other_w], axis=1), NT, preferred_element_type=F32
    )
    return both[:H], both[H:]


def plan(ptr1, cols1, ask, slot, tgt):
    col = lax.axis_index("col")
    n1 = cols1.shape[1]
    live = ptr1[ptr1.shape[0] - 1]
    names = cols1[...]
    lanes = lax.broadcasted_iota(I32, (1, n1), 1)
    owner = names >> 7
    hit = jnp.where(
        (lax.broadcasted_iota(I32, (16, n1), 0) == owner) & (lanes < live), 1.0, 0.0
    ).astype(F32)
    before = jnp.where(
        lax.broadcasted_iota(I32, (n1, n1), 0) < lax.broadcasted_iota(I32, (n1, n1), 1), 1.0, 0.0
    ).astype(BF16)
    count = jnp.dot(hit.astype(BF16), before, preferred_element_type=F32)
    rank = jnp.sum(hit * count, axis=0, keepdims=True)
    line = jnp.full((1, n1), 15, I32)
    for i in range(15):
        line = jnp.where(owner == at(col, ORDER[NEG[i]]), i, line)
    tgt[...] = jnp.where(lanes < live, line * 32 + rank.astype(I32), 0)
    place = jnp.where(
        lax.broadcasted_iota(I32, (E, n1), 0).astype(F32) == rank, 1.0, 0.0
    ).astype(BF16)
    listed = jnp.concatenate(
        [
            hit * (names & (E - 1)).astype(F32),
            hit * (lanes >> 8).astype(F32),
            hit * (lanes & 255).astype(F32),
        ],
        axis=0,
    ).astype(BF16)
    table = lax.dot_general(listed, place, NT, preferred_element_type=F32).astype(I32)
    for p in range(16):
        ask[p] = table[p : p + 1]
        spot = jnp.int32(15)
        for i in range(15):
            spot = jnp.where(at(col, ORDER[NEG[i]]) == p, i, spot)
        slot[spot] = table[16 + p : 17 + p] * 256 + table[32 + p : 33 + p]


def emit(parts, out1, out2, out3):
    first = 0
    for out in (out1, out2, out3):
        for i in range(out.shape[1] // E):
            out[:, i * E : (i + 1) * E] = jnp.concatenate(
                [parts[0, first + i], parts[1, first + i]], axis=0
            )
        first += out.shape[1] // E


def kernel(
    ask, pts1, pts2, pts3, s_tgt, s_slot, ptr1, cols2, ptr2, cols3, ptr3,
    fine_hbm, t1_hbm, t2_hbm, t3_hbm,
    parts_hbm,
    fine, blocks, t1, t2, t3,
    asked, s_asked,
    snd, got, prod, run,
    d_snd, d_got, own1, z_snd, z_got, inj1, g1a, g1b,
    c_snd, c_got, own2, inj2, g2a, g2b,
    r_snd, r_got, own3, out3,
    ld_sem, t_sem, ix_sem,
    ask_s, ask_r, rep_s, rep_r, d_s, d_r, z_s, z_r, a_s, a_r,
    p_s, p_r, q_s, q_r, m_s, m_r, o_sem,
):
    row = lax.axis_index("row")
    col = lax.axis_index("col")
    z, core = row // 2, lax.rem(row, 2)
    other = 1 - core
    partner = z * 2 + other
    g1, g2 = (g1a, g1b), (g2a, g2b)
    zero = jnp.zeros((H, E), F32)
    zs = [lax.rem(z + dz, 4) for dz in (1, 3, 2)]
    to = [at(col, offset) for offset in ORDER]
    back = [at(col, ORDER[NEG[i]]) for i in range(15)]

    def remote(src, dst, send, recv, **device):
        return pltpu.make_async_remote_copy(
            src_ref=src, dst_ref=dst, send_sem=send, recv_sem=recv,
            device_id=device, device_id_type=MESH,
        )

    load_fine = pltpu.make_async_copy(fine_hbm, fine, ld_sem.at[0])
    load_fine.start()
    load_t1 = pltpu.make_async_copy(t1_hbm, t1, t_sem.at[0])
    load_t1.start()
    load_t2 = pltpu.make_async_copy(t2_hbm, t2, t_sem.at[1])
    load_t3 = pltpu.make_async_copy(t3_hbm, t3, t_sem.at[2])

    barrier = pltpu.get_barrier_semaphore()
    for d in range(1, 16):
        pl.semaphore_signal(barrier, inc=1, device_id={"col": lax.rem(col + d, 16)}, device_id_type=MESH)
    for d in range(1, 8):
        pl.semaphore_signal(barrier, inc=1, device_id={"row": lax.rem(row + d, 8)}, device_id_type=MESH)
    pl.semaphore_wait(barrier, 22)

    asks = [remote(ask.at[to[i]], asked.at[i], ask_s.at[i], ask_r.at[i], col=to[i]) for i in range(15)]
    for copy in asks:
        copy.start()
    asked[15] = ask[col]
    load_fine.wait()

    def cut(j, carry):
        block = fine[:, pl.ds(pl.multiple_of(j * E, E), E)].astype(F32)
        blocks[0, j] = block[:H].astype(BF16)
        blocks[1, j] = block[H:].astype(BF16)
        return carry

    lax.fori_loop(0, 128, cut, 0, unroll=8)
    for copy in asks:
        copy.wait_recv()
    copy_asked = pltpu.make_async_copy(asked, s_asked, ix_sem.at[0])
    copy_asked.start()
    copy_asked.wait()

    def fill(h, target, i):
        def one(k, carry):
            target[k] = blocks[h, s_asked[i, 0, k]]
            return carry

        lax.fori_loop(0, 32, one, 0, unroll=16)

    def reply(h, i):
        return remote(snd.at[h, i], got.at[h, i], rep_s.at[h, i], rep_r.at[h, i], col=to[i])

    for h in range(2):
        for i in range(15):
            fill(h, snd.at[h, i], NEG[i])
            reply(h, i).start()
    for h in range(2):
        fill(h, got.at[h, 15], 15)
    load_t2.start()
    load_t3.start()

    def inject_one(first, last):
        def some(g, carry):
            def store(i, block):
                inj1[0, g * 8 + i] = block[:H]
                inj1[1, g * 8 + i] = block[H:]

            inject(lambda j: fine[:, pl.ds(pl.multiple_of(j * E, E), E)], 128, pts1, g * 8, 8, store)
            return carry

        lax.fori_loop(first, last, some, 0)

    def products(h, first, last):
        for i in range(first, min(last, 15)):
            reply(h, i).wait_recv()

        def one(n, carry):
            i, k = n // 16, lax.rem(n, 16) * 2
            t = i * 32 + k
            prod[t], prod[t + 1] = pair_products(
                got[h, i, k], got[h, i, k + 1], t1[s_slot[i, 0, k]], t1[s_slot[i, 0, k + 1]]
            )
            return carry

        lax.fori_loop(first * 16, last * 16, one, 0, unroll=16)

    def sums(ptr, b):
        return run[ptr[b + 1]] - run[ptr[b]]

    def to_partner(h, zt):
        return remote(d_snd.at[h, zt], d_got.at[h, zt], d_s.at[h, zt], d_r.at[h, zt], row=partner)

    def along_z(h, i):
        j = (1, 0, 2)[i]
        return remote(z_snd.at[h, i], z_got.at[h, j], z_s.at[h, i], z_r.at[h, j], row=zs[i] * 2 + core)

    def sum_one(h):
        run[0] = zero

        def add(s, total):
            total = total + prod[s_tgt[0, s]]
            run[s + 1] = total
            return total

        lax.fori_loop(0, t1.shape[0], add, zero, unroll=16)
        for zt in zs + [z]:

            def give(i, carry, zt=zt):
                d_snd[h, zt, i] = sums(ptr1, zt * 64 + other * 32 + i).astype(BF16)
                return carry

            lax.fori_loop(0, 32, give, 0, unroll=16)
            to_partner(h, zt).start()
        for zt in zs + [z]:

            def keep(i, carry, zt=zt):
                own1[h, zt, i] = sums(ptr1, zt * 64 + core * 32 + i)
                return carry

            lax.fori_loop(0, 32, keep, 0, unroll=16)

    def join(h):
        for n, zt in enumerate(zs):
            to_partner(h, zt).wait_recv()

            def add(i, carry, zt=zt, n=n):
                z_snd[h, n, i] = (own1[h, zt, i] + d_got[h, zt, i].astype(F32)).astype(BF16)
                return carry

            lax.fori_loop(0, 32, add, 0, unroll=16)
            along_z(h, n).start()
        to_partner(h, z).wait_recv()

    def piece(h, r):
        return g1[h].at[pl.ds(r * 32, 32)]

    def spread_z(h, i):
        return remote(piece(h, row), piece(h, row), a_s.at[h, i], a_r.at[h, row], row=zs[i] * 2 + core)

    def spread_chip(h, zt, i):
        r = zt * 2 + core
        return remote(piece(h, r), piece(h, r), a_s.at[h, 3 + i], a_r.at[h, r], row=partner)

    def arrival(h, r):
        return remote(piece(h, r), piece(h, r), a_s.at[h, 0], a_r.at[h, r], row=partner)

    def final_one(h):
        for i in range(3):
            along_z(h, i).wait_recv()

        def add(i, carry):
            total = (own1[h, z, i] + d_got[h, z, i].astype(F32)) + inj1[h, i]
            for n in range(3):
                total = total + z_got[h, n, i].astype(F32)
            g1[h][row * 32 + i] = total.astype(BF16)
            return carry

        lax.fori_loop(0, 32, add, 0, unroll=16)
        for i in range(3):
            spread_z(h, i).start()
        spread_chip(h, z, 3).start()
        pltpu.make_async_copy(piece(h, row), parts_hbm.at[h, pl.ds(0, 32)], o_sem.at[h, 0]).start()

        def store(i, block):
            inj2[h, i] = block

        inject(lambda j: g1[h][row * 32 + j], 32, pts2, 0, 8, store)

    def pass_on(h):
        for i, zt in enumerate(zs):
            arrival(h, zt * 2 + core).wait_recv()
            spread_chip(h, zt, i).start()

    def arrived(h):
        for zt in [z] + zs:
            arrival(h, zt * 2 + other).wait_recv()

    def tile_sums(vectors, tiles, columns):
        run[0] = zero

        def two(n, total):
            s = n * 2
            a, b = pair_products(vectors[columns[s]], vectors[columns[s + 1]], tiles[s], tiles[s + 1])
            a = total + a
            run[s + 1] = a
            b = a + b
            run[s + 2] = b
            return b

        lax.fori_loop(0, tiles.shape[0] // 2, two, zero, unroll=16)

    def part_two(h, i):
        return remote(c_snd.at[h, i], c_got.at[h, i], p_s.at[h, i], p_r.at[h, i], col=to[i])

    def level_two(h):
        tile_sums(g1[h], t2, cols2)
        for n in range(15):

            def give(i, carry, n=n):
                c_snd[h, n, i] = sums(ptr2, to[n] * 8 + i).astype(BF16)
                return carry

            lax.fori_loop(0, 8, give, 0, unroll=8)
            part_two(h, n).start()

        def keep(i, carry):
            own2[h, i] = sums(ptr2, col * 8 + i) + inj2[h, i]
            return carry

        lax.fori_loop(0, 8, keep, 0, unroll=8)

    def spread_two(h, i):
        mine = g2[h].at[pl.ds(col * 8, 8)]
        return remote(mine, mine, q_s.at[h, i], q_r.at[h, i], col=to[i])

    def final_two(h):
        for i in range(15):
            part_two(h, i).wait_recv()

        def add(i, carry):
            total = own2[h, i]
            for n in range(15):
                total = total + c_got[h, n, i].astype(F32)
            g2[h][col * 8 + i] = total.astype(BF16)
            return carry

        lax.fori_loop(0, 8, add, 0, unroll=4)
        for i in range(15):
            spread_two(h, i).start()
        pltpu.make_async_copy(
            g2[h].at[pl.ds(col * 8, 8)], parts_hbm.at[h, pl.ds(32, 8)], o_sem.at[h, 1]
        ).start()

        def store(i, block):
            own3[h, i] = block

        inject(lambda j: g2[h][col * 8 + j], 8, pts3, 0, 2, store)

    def part_three(h, d):
        peer = lax.rem(row + d, 8)
        return remote(r_snd.at[h, d], r_got.at[h, d], m_s.at[h, d], m_r.at[h, d], row=peer)

    def level_three(h):
        for i in range(15):
            there = g2[h].at[pl.ds(back[i] * 8, 8)]
            remote(there, there, q_s.at[h, i], q_r.at[h, i], col=to[i]).wait_recv()
        tile_sums(g2[h], t3, cols3)
        for d in range(1, 8):
            peer = lax.rem(row + d, 8)
            for i in range(2):
                r_snd[h, d, i] = sums(ptr3, peer * 2 + i)
            part_three(h, d).start()
        for i in range(2):
            own3[h, i] = own3[h, i] + sums(ptr3, row * 2 + i)

    def final_three(h):
        for d in range(1, 8):
            part_three(h, d).wait_recv()
        for i in range(2):
            total = own3[h, i]
            for d in range(1, 8):
                total = total + r_got[h, d, i]
            out3[h, i] = total.astype(BF16)
        pltpu.make_async_copy(out3.at[h], parts_hbm.at[h, pl.ds(40, 2)], o_sem.at[h, 2]).start()

    A, B = 0, 1
    inject_one(0, 2)
    load_t1.wait()
    products(A, 0, 5)
    products(A, 5, 10)
    products(A, 10, 14)
    products(A, 14, 16)
    sum_one(A)
    products(B, 0, 3)
    join(A)
    inject_one(2, 4)
    final_one(A)
    products(B, 3, 9)
    products(B, 9, 14)
    pass_on(A)
    products(B, 14, 16)
    sum_one(B)
    join(B)
    load_t2.wait()
    arrived(A)
    level_two(A)
    final_one(B)
    final_two(A)
    pass_on(B)
    arrived(B)
    load_t3.wait()
    level_two(B)
    level_three(A)
    final_two(B)
    level_three(B)
    final_three(A)
    final_three(B)

    for copy in asks:
        copy.wait_send()
    for h in range(2):
        for i in range(15):
            reply(h, i).wait_send()
            part_two(h, i).wait_send()
            spread_two(h, i).wait_send()
        for zt in range(4):
            to_partner(h, zt).wait_send()
        for i, zt in enumerate(zs + [z]):
            spread_chip(h, zt, i).wait_send()
        for i in range(3):
            along_z(h, i).wait_send()
            spread_z(h, i).wait_send()
        for d in range(1, 8):
            part_three(h, d).wait_send()
        pltpu.make_async_copy(piece(h, row), parts_hbm.at[h, pl.ds(0, 32)], o_sem.at[h, 0]).wait()
        pltpu.make_async_copy(
            g2[h].at[pl.ds(col * 8, 8)], parts_hbm.at[h, pl.ds(32, 8)], o_sem.at[h, 1]
        ).wait()
        pltpu.make_async_copy(out3.at[h], parts_hbm.at[h, pl.ds(40, 2)], o_sem.at[h, 2]).wait()


def on_device(
    fine, tiles1, ptr1, cols1, pts1, tiles2, ptr2, cols2, pts2, tiles3, ptr3, cols3, pts3
):
    n1 = tiles1.shape[0]
    hbm = pl.BlockSpec(memory_space=pl.ANY)
    vmem = pl.BlockSpec(memory_space=pltpu.VMEM)
    smem = pl.BlockSpec(memory_space=pltpu.SMEM)
    dma = pltpu.SemaphoreType.DMA
    vm = pltpu.VMEM
    ask, slot, tgt = pl.pallas_call(
        plan,
        out_shape=[
            jax.ShapeDtypeStruct((16, 1, E), I32),
            jax.ShapeDtypeStruct((16, 1, E), I32),
            jax.ShapeDtypeStruct((1, n1), I32),
        ],
        in_specs=[smem, vmem],
        out_specs=[vmem] * 3,
        name="plan",
    )(ptr1, cols1.reshape(1, n1))
    scratch = [
        vm(fine.shape, BF16), vm((2, 128, H, E), BF16), vm(tiles1.shape, BF16), vm(tiles2.shape, BF16), vm(tiles3.shape, BF16),
        vm((16, 1, E), I32), pltpu.SMEM((16, 1, E), I32),
        vm((2, 15, 32, H, E), BF16), vm((2, 16, 32, H, E), BF16), vm((n1, H, E), F32), vm((n1 + 1, H, E), F32),
        vm((2, 4, 32, H, E), BF16), vm((2, 4, 32, H, E), BF16), vm((2, 4, 32, H, E), F32),
        vm((2, 3, 32, H, E), BF16), vm((2, 3, 32, H, E), BF16), vm((2, 32, H, E), F32), vm((256, H, E), BF16), vm((256, H, E), BF16),
        vm((2, 15, 8, H, E), BF16), vm((2, 15, 8, H, E), BF16), vm((2, 8, H, E), F32), vm((2, 8, H, E), F32), vm((128, H, E), BF16), vm((128, H, E), BF16),
        vm((2, 8, 2, H, E), F32), vm((2, 8, 2, H, E), F32), vm((2, 2, H, E), F32), vm((2, 2, H, E), BF16),
        dma((1,)), dma((3,)), dma((1,)),
        dma((15,)), dma((15,)), dma((2, 15)), dma((2, 15)), dma((2, 4)), dma((2, 4)), dma((2, 3)), dma((2, 3)), dma((2, 7)), dma((2, 8)),
        dma((2, 15)), dma((2, 15)), dma((2, 15)), dma((2, 15)), dma((2, 8)), dma((2, 8)), dma((2, 3)),
    ]
    parts = pl.pallas_call(
        kernel,
        out_shape=jax.ShapeDtypeStruct((2, 42, H, E), BF16),
        in_specs=[vmem] * 4 + [smem] * 7 + [hbm] * 4,
        out_specs=hbm,
        scratch_shapes=scratch,
        compiler_params=pltpu.CompilerParams(
            collective_id=0, has_side_effects=True, vmem_limit_bytes=58 << 20
        ),
        name="restrict",
    )(
        ask, pts1.reshape(-1, E), pts2.reshape(-1, E), pts3.reshape(-1, E),
        tgt, slot, ptr1, cols2, ptr2, cols3, ptr3, fine, tiles1, tiles2, tiles3,
    )
    return pl.pallas_call(
        emit,
        out_shape=tuple(
            jax.ShapeDtypeStruct((V, points.shape[0]), BF16) for points in (pts1, pts2, pts3)
        ),
        in_specs=[vmem],
        out_specs=(vmem,) * 3,
        name="emit",
    )(parts)


def solution(mesh):
    placed = (
        P(None, ("row", "col")),
        P(("row", "col"), None, None),
        P(("row", "col")),
        P(("row", "col")),
        P(("col", "row")),
        P(("row", "col"), None, None),
        P(("row", "col")),
        P(("row", "col")),
        P(("row", "col")),
        P(("row", "col"), None, None),
        P(("row", "col")),
        P(("row", "col")),
        P(("col", "row")),
    )
    return jax.shard_map(
        on_device,
        mesh=mesh,
        in_specs=placed,
        out_specs=(P(None, ("col", "row")), P(None, ("row", "col")), P(None, ("col", "row"))),
        check_vma=False,
    )
```

time: 109 us -> 93.9 us (0.86)
  Pallas kernels: 104 us -> 93 us
  local copies, waits for them, and re-layouts: 4.24 us -> 0 us
    pallas_call x1 -> x2, Pallas kernels: 102 us -> 91.3 us  [the longest x1 89.7 us: on_device(): pl.pallas_call(kernel, out_shape=jax.ShapeDtypeStruct((2, 42, H, E), BF16...]
    unnamed x3 -> x0, local copies, waits for them, and re-layouts: 4.24 us -> none
where the time goes in v2:
time: 93.9 us; the launch traced here: 93.7 us
  Pallas kernels  93 us (99%)
    pallas_call x1, Pallas kernels, on_device(): pl.pallas_call(kernel, out_shape=jax.ShapeDtypeStruct((2, 42, H, E), BF16...  89.7 us

profile of v2, /device:TPU:1, one launch (start us, length us, event | category | flops | bytes accessed | tf_op | source)
XLA Modules:
  0.0 93.7 jit_solution(8228238785733539566)
XLA Ops:
  0.6 1.7 %plan.1 = (s32[16,1,128]{2,1,0:T(1,128)}, s32[16,1,128]{2,1,0:T(1,128)}, s32[1,512]{1,0:T(1,128)}) custom-call(s32[257]{0:T(512)} %ptr1.3, s32[1,512]{1,0:T(1,128)} %bitcast.6), custom_call_target="tpu_custom_call" | custom-call | tf_op jit(solution)/shard_map/plan/pallas_call | solution.py:464
  2.3 89.7 %restrict.1.parts = bf16[2,42,8,128]{3,2,1,0:T(8,128)(2,1)} custom-call(s32[16,1,128]{2,1,0:T(1,128)} %get-tuple-element.6.ask, s32[32,128]{1,0:T(8,128)} %bitcast.4, s32[8,128]{1,0:T(8,128)} %bitcast.5, s32[2,128]{1,0:T(2,128)} %bitcast.7, s32[1,512]{1,0:T(1,128)} %get-tuple-element.7.s_tgt, s32[16,1,128]{2,1,0:T(1,128)} %get-tuple-element.8.s_slot, ...), custom_call_target="tpu_custom_call" | custom-call | tf_op jit(solution)/shard_map/restrict/pallas_call | solution.py:487
  92.1 1.6 %emit.1 = (bf16[16,4096]{1,0:T(8,128)(2,1)}, bf16[16,1024]{1,0:T(8,128)(2,1)}, bf16[16,256]{1,0:T(8,128)(2,1)}) custom-call(bf16[2,42,8,128]{3,2,1,0:T(8,128)(2,1)} %restrict.1.parts), custom_call_target="tpu_custom_call" | custom-call | tf_op jit(solution)/shard_map/emit/pallas_call | solution.py:501

commit v3 on v2

--- a/solution.py
+++ b/solution.py
@@ -114,7 +114,7 @@
     fine_hbm, t1_hbm, t2_hbm, t3_hbm,
     parts_hbm,
     fine, blocks, t1, t2, t3,
-    asked, s_asked,
+    s_asked,
     snd, got, prod, run,
     d_snd, d_got, own1, z_snd, z_got, inj1, g1a, g1b,
     c_snd, c_got, own2, inj2, g2a, g2b,
@@ -154,10 +154,11 @@
         pl.semaphore_signal(barrier, inc=1, device_id={"row": lax.rem(row + d, 8)}, device_id_type=MESH)
     pl.semaphore_wait(barrier, 22)
 
-    asks = [remote(ask.at[to[i]], asked.at[i], ask_s.at[i], ask_r.at[i], col=to[i]) for i in range(15)]
+    asks = [remote(ask.at[to[i]], s_asked.at[i], ask_s.at[i], ask_r.at[i], col=to[i]) for i in range(15)]
     for copy in asks:
         copy.start()
-    asked[15] = ask[col]
+    own_ask = pltpu.make_async_copy(ask.at[col], s_asked.at[15], ix_sem.at[0])
+    own_ask.start()
     load_fine.wait()
 
     def cut(j, carry):
@@ -169,9 +170,7 @@
     lax.fori_loop(0, 128, cut, 0, unroll=8)
     for copy in asks:
         copy.wait_recv()
-    copy_asked = pltpu.make_async_copy(asked, s_asked, ix_sem.at[0])
-    copy_asked.start()
-    copy_asked.wait()
+    own_ask.wait()
 
     def fill(h, target, i):
         def one(k, carry):
@@ -397,7 +396,7 @@
         pltpu.make_async_copy(out3.at[h], parts_hbm.at[h, pl.ds(40, 2)], o_sem.at[h, 2]).start()
 
     A, B = 0, 1
-    inject_one(0, 2)
+    inject_one(0, 3)
     load_t1.wait()
     products(A, 0, 5)
     products(A, 5, 10)
@@ -406,20 +405,20 @@
     sum_one(A)
     products(B, 0, 3)
     join(A)
-    inject_one(2, 4)
+    inject_one(3, 4)
     final_one(A)
     products(B, 3, 9)
     products(B, 9, 14)
-    pass_on(A)
     products(B, 14, 16)
     sum_one(B)
+    pass_on(A)
     join(B)
     load_t2.wait()
     arrived(A)
     level_two(A)
     final_one(B)
+    pass_on(B)
     final_two(A)
-    pass_on(B)
     arrived(B)
     load_t3.wait()
     level_two(B)
@@ -474,7 +473,7 @@
     )(ptr1, cols1.reshape(1, n1))
     scratch = [
         vm(fine.shape, BF16), vm((2, 128, H, E), BF16), vm(tiles1.shape, BF16), vm(tiles2.shape, BF16), vm(tiles3.shape, BF16),
-        vm((16, 1, E), I32), pltpu.SMEM((16, 1, E), I32),
+        pltpu.SMEM((16, 1, E), I32),
         vm((2, 15, 32, H, E), BF16), vm((2, 16, 32, H, E), BF16), vm((n1, H, E), F32), vm((n1 + 1, H, E), F32),
         vm((2, 4, 32, H, E), BF16), vm((2, 4, 32, H, E), BF16), vm((2, 4, 32, H, E), F32),
         vm((2, 3, 32, H, E), BF16), vm((2, 3, 32, H, E), BF16), vm((2, 32, H, E), F32), vm((256, H, E), BF16), vm((256, H, E), BF16),

time: 93.9 us -> 90.2 us (0.961)
  Pallas kernels: 93 us -> 89.4 us
    pallas_call x1, Pallas kernels: 89.7 us -> 86 us  [on_device(): pl.pallas_call(kernel, out_shape=jax.ShapeDtypeStruct((2, 42, H, E), BF16...]
where the time goes in v3:
time: 90.2 us; the launch traced here: 90 us
  Pallas kernels  89.4 us (99%)
    pallas_call x1, Pallas kernels, on_device(): pl.pallas_call(kernel, out_shape=jax.ShapeDtypeStruct((2, 42, H, E), BF16...  86 us

profile of v3, /device:TPU:1, one launch (start us, length us, event | category | flops | bytes accessed | tf_op | source)
XLA Modules:
  0.0 90.0 jit_solution(16870155061783945457)
XLA Ops:
  0.6 1.7 %plan.1 = (s32[16,1,128]{2,1,0:T(1,128)}, s32[16,1,128]{2,1,0:T(1,128)}, s32[1,512]{1,0:T(1,128)}) custom-call(s32[257]{0:T(512)} %ptr1.3, s32[1,512]{1,0:T(1,128)} %bitcast.6), custom_call_target="tpu_custom_call" | custom-call | tf_op jit(solution)/shard_map/plan/pallas_call | solution.py:463
  2.3 86.0 %restrict.1.parts = bf16[2,42,8,128]{3,2,1,0:T(8,128)(2,1)} custom-call(s32[16,1,128]{2,1,0:T(1,128)} %get-tuple-element.6.ask, s32[32,128]{1,0:T(8,128)} %bitcast.4, s32[8,128]{1,0:T(8,128)} %bitcast.5, s32[2,128]{1,0:T(2,128)} %bitcast.7, s32[1,512]{1,0:T(1,128)} %get-tuple-element.7.s_tgt, s32[16,1,128]{2,1,0:T(1,128)} %get-tuple-element.8.s_slot, ...), custom_call_target="tpu_custom_call" | custom-call | tf_op jit(solution)/shard_map/restrict/pallas_call | solution.py:486
  88.4 1.6 %emit.1 = (bf16[16,4096]{1,0:T(8,128)(2,1)}, bf16[16,1024]{1,0:T(8,128)(2,1)}, bf16[16,256]{1,0:T(8,128)(2,1)}) custom-call(bf16[2,42,8,128]{3,2,1,0:T(8,128)(2,1)} %restrict.1.parts), custom_call_target="tpu_custom_call" | custom-call | tf_op jit(solution)/shard_map/emit/pallas_call | solution.py:500

commit v4 on v3

--- a/solution.py
+++ b/solution.py
@@ -396,7 +396,7 @@
         pltpu.make_async_copy(out3.at[h], parts_hbm.at[h, pl.ds(40, 2)], o_sem.at[h, 2]).start()
 
     A, B = 0, 1
-    inject_one(0, 3)
+    inject_one(0, 4)
     load_t1.wait()
     products(A, 0, 5)
     products(A, 5, 10)
@@ -405,7 +405,6 @@
     sum_one(A)
     products(B, 0, 3)
     join(A)
-    inject_one(3, 4)
     final_one(A)
     products(B, 3, 9)
     products(B, 9, 14)

time: 90.2 us -> 94.2 us (1.044)
  Pallas kernels: 89.4 us -> 93.3 us
    pallas_call x1, Pallas kernels: 86 us -> 90 us  [on_device(): pl.pallas_call(kernel, out_shape=jax.ShapeDtypeStruct((2, 42, H, E), BF16...]
where the time goes in v4:
time: 94.2 us; the launch traced here: 93.9 us
  Pallas kernels  93.3 us (99%)
    pallas_call x1, Pallas kernels, on_device(): pl.pallas_call(kernel, out_shape=jax.ShapeDtypeStruct((2, 42, H, E), BF16...  90 us

profile of v4, /device:TPU:1, one launch (start us, length us, event | category | flops | bytes accessed | tf_op | source)
XLA Modules:
  0.0 93.9 jit_solution(12473163768521518408)
XLA Ops:
  0.6 1.7 %plan.1 = (s32[16,1,128]{2,1,0:T(1,128)}, s32[16,1,128]{2,1,0:T(1,128)}, s32[1,512]{1,0:T(1,128)}) custom-call(s32[257]{0:T(512)} %ptr1.3, s32[1,512]{1,0:T(1,128)} %bitcast.6), custom_call_target="tpu_custom_call" | custom-call | tf_op jit(solution)/shard_map/plan/pallas_call | solution.py:462
  2.3 90.0 %restrict.1.parts = bf16[2,42,8,128]{3,2,1,0:T(8,128)(2,1)} custom-call(s32[16,1,128]{2,1,0:T(1,128)} %get-tuple-element.6.ask, s32[32,128]{1,0:T(8,128)} %bitcast.4, s32[8,128]{1,0:T(8,128)} %bitcast.5, s32[2,128]{1,0:T(2,128)} %bitcast.7, s32[1,512]{1,0:T(1,128)} %get-tuple-element.7.s_tgt, s32[16,1,128]{2,1,0:T(1,128)} %get-tuple-element.8.s_slot, ...), custom_call_target="tpu_custom_call" | custom-call | tf_op jit(solution)/shard_map/restrict/pallas_call | solution.py:485
  92.3 1.6 %emit.1 = (bf16[16,4096]{1,0:T(8,128)(2,1)}, bf16[16,1024]{1,0:T(8,128)(2,1)}, bf16[16,256]{1,0:T(8,128)(2,1)}) custom-call(bf16[2,42,8,128]{3,2,1,0:T(8,128)(2,1)} %restrict.1.parts), custom_call_target="tpu_custom_call" | custom-call | tf_op jit(solution)/shard_map/emit/pallas_call | solution.py:499
